TPU v7x, 32 devices: a whole 2x2x4 slice. The times are simulated.
32 devices in a mesh: cls: 4 (over y, x), org: 8 (over z, core).
Axes of the slice: x: 2, y: 2, z: 4, core: 2. Of those that a mesh axis runs over, the one named last changes fastest.
Arguments:
- flows_start: float32 [8, 49152], P('cls', 'org'), may hold values from 150 to 300
- interaction: float32 [8, 8, 49152], P('cls', None, 'org'), may hold values from 0.2 to 2
- free_time: float32 [8, 49152], P('cls', 'org'), may hold values from 0.01 to 0.1
- capacity: float32 [49152], P('org'), may hold values from 300 to 900
- demand: int32 [8, 8, 60], P('cls', 'org'), may hold values from 0 to 15
- incidence: int32 [2, 8, 8, 2, 49152], P(None, 'cls', 'org'), may hold values from 0 to 1073741823, as said below
- step_size: float32 [2], replicated, may hold values from 0.3 to 0.6
Outputs:
- flows: float32 [8, 49152], P('cls', 'org')
- costs: float32 [8, 49152], P('cls', 'org')
- skims: float32 [2, 8, 8, 60], P(None, 'cls', 'org')
- gaps: float32 [2], replicated
Inputs may be any that keep to these rules, and one draw needn't show every extreme that they name: Bit b of incidence[k, c, o, w, l] tells whether link l lies on class c's path from anchor o to destination w * 30 + b in iteration k; each path is the union of 4 runs of 64 consecutive links (counted cyclically over the links) at drawn starts, the first of which is shared by all 30 destinations of one word.
All inputs are finite; a program needn't handle non-finite values.
Results may differ from a plain program's by a relative error of at most 0.0013.
Values sent between devices are 32-bit elements; how exact they have to be, the bound alone decides.
A program may use at most 256 MiB of HBM per device.

v0:
```python
import jax
import jax.numpy as jnp
from jax import lax
from jax.sharding import PartitionSpec as P

BITS = 30
ITERS = 2
HIGH = lax.Precision.HIGHEST


def unpack_half(packed):
    shifts = jnp.arange(BITS, dtype=jnp.int32)
    bit_table = jnp.bitwise_and(jnp.right_shift(packed[..., :, None, :], shifts[:, None]), 1)
    new_shape = packed.shape[:-2] + (packed.shape[-2] * BITS, packed.shape[-1])
    return bit_table.reshape(new_shape).astype(jnp.bfloat16)


def link_cost(flows_all, inter, free, cap):
    load_sum = jnp.einsum("cel,el->cl", inter, flows_all, precision=HIGH)
    load_ratio = load_sum / cap
    square = load_ratio * load_ratio
    return free * (1.0 + 0.15 * square * square)


def split_three(values):
    upper = values.astype(jnp.bfloat16)
    remain = values - upper.astype(jnp.float32)
    middle = remain.astype(jnp.bfloat16)
    lowest = (remain - middle.astype(jnp.float32)).astype(jnp.bfloat16)
    return jnp.stack([upper, middle, lowest], axis=1)


def skim_block(bit_table, cost_block):
    parts = split_three(cost_block)
    terms = jnp.einsum("codl,cpl->cpod", bit_table, parts, preferred_element_type=jnp.float32)
    return jnp.sum(terms, axis=1)


def anchor_loads_local(packed_all, trips_half, link_shard, block_count):

    def one_block(block_index):
        word_block = lax.dynamic_slice_in_dim(packed_all, block_index * link_shard, link_shard, 3)
        bit_table = unpack_half(word_block)
        return jnp.einsum("cod,codl->cl", trips_half, bit_table, preferred_element_type=jnp.float32)

    blocks = lax.map(one_block, jnp.arange(block_count, dtype=jnp.int32))
    return jnp.moveaxis(blocks, 0, 1).reshape(blocks.shape[1], block_count * link_shard)


def make_fold(packed_all, link_shard):

    def fold_links(skim_carry, portion, first):
        turn_count = portion.shape[1] // link_shard

        def advance(skim_sum, block_index):
            offset = block_index * link_shard
            word_block = lax.dynamic_slice_in_dim(packed_all, offset, link_shard, 3)
            bit_table = unpack_half(word_block)
            cost_block = lax.dynamic_slice_in_dim(portion, offset, link_shard, 1)
            return (skim_sum + skim_block(bit_table, cost_block), None)

        result, unused = lax.scan(advance, skim_carry, jnp.arange(turn_count, dtype=jnp.int32))
        return result

    return fold_links


def both_totals(cost_part, path_part):
    return lax.psum((cost_part, path_part), ("cls", "org"))


def shards(flows_start, interaction, free_time, capacity, demand, incidence, step_size):
    org_count = lax.axis_size("org")
    link_shard = flows_start.shape[1]
    dest_count = demand.shape[2]
    class_local = demand.shape[0]
    demand_real = demand.astype(jnp.float32)
    trips_half = demand.astype(jnp.bfloat16)
    own_start = lax.axis_index("org") * link_shard
    skim_init = jnp.zeros((class_local, demand.shape[1], dest_count), jnp.float32)
    skim_list = []
    gap_list = []
    inter_full, free_full, cap_full, flow_now = (
        lax.all_gather(interaction, "org", axis=2, tiled=True),
        lax.all_gather(free_time, "org", axis=1, tiled=True),
        lax.all_gather(capacity, "org", axis=0, tiled=True),
        lax.all_gather(flows_start, "org", axis=1, tiled=True),
    )

    def full_cost(flow_value):
        flows_all = lax.all_gather(flow_value, "cls", axis=0, tiled=True)
        return link_cost(flows_all, inter_full, free_full, cap_full)

    for iteration in range(ITERS):
        cost_now = full_cost(flow_now)
        fold_links = make_fold(incidence[iteration], link_shard)
        skim_now = fold_links(skim_init, cost_now, jnp.int32(0))
        partial_value = anchor_loads_local(incidence[iteration], trips_half, link_shard, org_count)
        aon = lax.psum(partial_value, "org")
        product = lax.dynamic_slice_in_dim(cost_now * flow_now, own_start, link_shard, 1)
        cost_total, path_total = both_totals(jnp.sum(product), jnp.sum(demand_real * skim_now))
        gap_list.append((cost_total - path_total) / cost_total)
        skim_list.append(skim_now)
        flow_now = flow_now + step_size[iteration] * (aon - flow_now)
    cost_final = full_cost(flow_now)
    flow_out = lax.dynamic_slice_in_dim(flow_now, own_start, link_shard, 1)
    cost_out = lax.dynamic_slice_in_dim(cost_final, own_start, link_shard, 1)
    return (flow_out, cost_out, jnp.stack(skim_list), jnp.stack(gap_list))


def solution(mesh):
    placed = (
        P("cls", "org"),
        P("cls", None, "org"),
        P("cls", "org"),
        P("org"),
        P("cls", "org", None),
        P(None, "cls", "org", None, None),
        P(),
    )
    return jax.shard_map(
        shards,
        mesh=mesh,
        in_specs=placed,
        out_specs=(P("cls", "org"), P("cls", "org"), P(None, "cls", "org", None), P()),
        check_vma=False,
    )
```

profile of v0, /device:TPU:0, one launch (start us, length us, event | category | flops | bytes accessed | tf_op | source)
XLA Modules:
  0.0 387.4 jit_solution(10713880894416797273)
XLA Ops:
  10.9 32.3 %while.43 = (s32[]{:T(128)}, f32[8,2,6144]{2,1,0:T(2,128)S(1)}, s32[8]{0:T(128)S(1)}, s32[2,1,2,49152]{3,0,2,1:T(2,128)S(1)}, bf16[2,1,60]{2,0,1:T(2,128)(2,1)S(...) while((s32[]{:T(128)}, f32[8,2,6144]{2,1,0:T(2,128)S(1)}, s32[8]{0:T(128)S(1)}, ...), condition=%wide.region_4.5_spmd, body=%wide.region_3.4_spmd.sunk | while | flops 3686406 | bytes 3392847 | solution.py:46
  12.3 1.7 fusion.83
  16.3 1.7 fusion.83
  20.3 1.7 fusion.83
  24.4 1.7 fusion.83
  28.4 1.7 fusion.83
  32.5 1.7 fusion.83
  36.5 1.7 fusion.83
  40.5 1.7 fusion.83
  44.3 32.3 %while.42 = (s32[]{:T(128)}, f32[8,2,6144]{2,1,0:T(2,128)S(1)}, s32[8]{0:T(128)S(1)}, s32[2,1,2,49152]{3,0,2,1:T(2,128)S(1)}, bf16[2,1,60]{2,0,1:T(2,128)(2,1)S(...) while((s32[]{:T(128)}, f32[8,2,6144]{2,1,0:T(2,128)S(1)}, s32[8]{0:T(128)S(1)}, ...), condition=%wide.region_1.0_spmd, body=%wide.region_0.1_spmd.sunk | while | flops 3686406 | bytes 3392847 | solution.py:46
  45.7 1.7 fusion.79
  49.7 1.7 fusion.79
  53.8 1.7 fusion.79
  57.8 1.7 fusion.79
  61.8 1.7 fusion.79
  65.9 1.7 fusion.79
  69.9 1.7 fusion.79
  74.0 1.7 fusion.79
  77.5 17.5 %all_gather.21 = f32[2,49152]{1,0:T(2,128)} all-gather(f32[2,6144]{1,0:T(2,128)S(1)} %copy-done.7), channel_id=1, replica_groups=mesh['cls'=4,'org'=8] {'org'}, dimensions={1}, use_global_device_ids=true | all-gather | bytes 442368 | tf_op jit(solution)/shard_map/all_gather | solution.py:87
  95.7 42.7 %all-reduce.4.cloned.1.call-done = (f32[2,49152]{1,0:T(2,128)}, f32[2,49152]{1,0:T(2,128)}) async-done(((f32[2,49152]{1,0:T(2,128)}, f32[2,49152]{1,0:T(2,128)}), (f32[2,49152]{1,0:T(2,128)}, f32[2,49152]{1,0:T(2,128)})) %all-reduce.4.cloned.1.call-update) | async-done | bytes 786448 | tf_op jit(solution)/shard_map/psum | solution.py:99
  138.4 3.8 multiply_add_fusion
  143.5 15.2 %all_gather.25 = f32[49152]{0:T(1024)} all-gather(f32[6144]{0:T(1024)S(1)} %copy-done.9), channel_id=1, replica_groups=mesh['cls'=4,'org'=8] {'org'}, dimensions={0}, use_global_device_ids=true | all-gather | bytes 221184 | tf_op jit(solution)/shard_map/all_gather | solution.py:86
  158.7 14.7 %all_gather.22 = f32[2,49152]{1,0:T(2,128)S(1)} all-gather(f32[2,6144]{1,0:T(2,128)S(1)} %copy-done.8), channel_id=1, replica_groups=mesh['cls'=4,'org'=8] {'org'}, dimensions={1}, use_global_device_ids=true | all-gather | bytes 442368 | tf_op jit(solution)/shard_map/all_gather | solution.py:85
  174.8 2.5 reshape.94
  177.3 2.5 reshape.92
  179.8 24.8 %all-gather.14.cloned.1.call-done = f32[4,2,49152]{2,1,0:T(2,128)} async-done(((f32[1,2,49152]{2,1,0:T(2,128)}), f32[4,2,49152]{2,1,0:T(2,128)}) %all-gather.14.cloned.1.call-update) | async-done | bytes 1572880 | tf_op jit(solution)/shard_map/all_gather | solution.py:91
  204.6 3.6 reshape.96
  208.2 36.0 %all-gather.8.cloned.1.call-done = f32[2,8,49152]{2,1,0:T(8,128)} async-done(((f32[2,8,6144]{2,1,0:T(8,128)}), f32[2,8,49152]{2,1,0:T(8,128)}) %all-gather.8.cloned.1.call-update) | async-done | bytes 3145744 | tf_op jit(solution)/shard_map/all_gather | solution.py:84
  244.2 6.9 %multiply_reduce_fusion.1 = (f32[49152,2]{0,1:T(2,128)S(1)}, f32[49152,2]{0,1:T(2,128)S(1)}, f32[49152,2]{0,1:T(2,128)}) fusion(f32[2,8,49152]{2,1,0:T(8,128)} %all-gather.8.cloned.1.call-done, f32[49152,8]{0,1:T(8,128)S(1)} %bitcast.155, f32[49152,8]{0,1:T(8,128)} %bitcast.157, f32[49152,8]{0,1:T(8,128)S(1)} %bitcast.156), kind=kLoop, calls=%fused_computation.59 | loop fusion | flops 4423680 | bytes 9043968 | tf_op jit(solution)/shard_map/cel,el->cl/dot_general | solution.py:19
  253.4 39.4 %while.44 = (s32[]{:T(128)}, f32[2,1,60]{2,0,1:T(2,128)S(1)}, s32[8]{0:T(128)S(1)}, f32[2,49152]{1,0:T(2,128)S(1)}, s32[2,1,2,49152]{3,0,2,1:T(2,128)}, /*index=5*/s32[]{:T(128)}, s32[1]{0:T(128)}, s32[]{:T(128)}, s32[]{:T(128)}) while((s32[]{:T(128)}, f32[2,1,60]{2,0,1:T(2,128)S(1)}, s32[8]{0:T(128)S(1)}, ...), condition=%wide.region_8.9_spmd.clone, body=%wide.region_6.8_spmd.clone.sunk | while | flops 6943207 | bytes 3615725 | solution.py:62
  294.2 39.4 %while.45 = (s32[]{:T(128)}, f32[2,1,60]{2,0,1:T(2,128)S(1)}, s32[8]{0:T(128)S(1)}, f32[2,49152]{1,0:T(2,128)S(1)}, s32[2,1,2,49152]{3,0,2,1:T(2,128)}, /*index=5*/s32[]{:T(128)}, s32[1]{0:T(128)}, s32[]{:T(128)}, s32[]{:T(128)}) while((s32[]{:T(128)}, f32[2,1,60]{2,0,1:T(2,128)S(1)}, s32[8]{0:T(128)S(1)}, ...), condition=%wide.region_11.12_spmd.clone, body=%wide.region_9.11_spmd.clone.sunk | while | flops 6943207 | bytes 3615725 | solution.py:62
  334.2 39.7 %all-reduce = (f32[]{:T(128)}, f32[]{:T(128)}, f32[]{:T(128)}, f32[]{:T(128)}) all-reduce(f32[]{:T(128)} %fusion.53, f32[]{:T(128)} %get-tuple-element.186, f32[]{:T(128)} %fusion.54, f32[]{:T(128)} %get-tuple-element.185), channel_id=1, replica_groups=mesh['cls'=4,'org'=8] {'cls','org'}, use_global_device_ids=true, to_apply=%region_17.18 | all-reduce | flops 4 | bytes 32 | tf_op jit(solution)/shard_map/psum | solution.py:69
  (345 shorter events, 107.4 us)
Async XLA Ops:
  8.0 130.4 %all-reduce.4.cloned.1.call-start = ((), (), s32[]{:S(2)}) async-start(), calls=%async_computation.4 | async-start | bytes 1572864 | tf_op jit(solution)/shard_map/psum | solution.py:99
  8.0 1.5 copy-start.11
  43.2 1.0 copy-start
  43.2 1.1 copy-start.6
  43.3 34.1 %copy-start.7 = (f32[2,6144]{1,0:T(2,128)S(1)}, f32[2,6144]{1,0:T(2,128)}, u32[]{:S(2)}) copy-start(f32[2,6144]{1,0:T(2,128)} %param.15) | copy-start | bytes 147460
  76.6 0.8 copy-start.5
  76.6 65.5 %copy-start.1 = (s32[2,1,2,49152]{3,0,2,1:T(2,128)}, s32[2,1,2,49152]{3,0,2,1:T(2,128)S(1)}, u32[]{:S(2)}) copy-start(s32[2,1,2,49152]{3,0,2,1:T(2,128)S(1)} %get-tuple-element.496) | copy-start | bytes 2359300
  76.6 18.4 %copy-start.10 = (f32[2]{0:T(128)S(1)}, f32[2]{0:T(128)}, u32[]{:S(2)}) copy-start(f32[2]{0:T(128)} %param.21) | copy-start | bytes 28
  77.4 97.4 %all-gather.12.cloned.1.call-start = ((), (), s32[]{:S(2)}) async-start(), calls=%async_computation.2 | async-start | bytes 1966080 | tf_op jit(solution)/shard_map/all_gather | solution.py:91
  95.0 82.3 %all-gather.10.cloned.1.call-start = ((), (), s32[]{:S(2)}) async-start(), calls=%async_computation.1 | async-start | bytes 1966080 | tf_op jit(solution)/shard_map/all_gather | solution.py:91
  138.4 5.1 %copy-start.9 = (f32[6144]{0:T(1024)S(1)}, f32[6144]{0:T(1024)}, u32[]{:S(2)}) copy-start(f32[6144]{0:T(1024)} %param.18) | copy-start | bytes 73732
  138.4 20.3 %copy-start.8 = (f32[2,6144]{1,0:T(2,128)S(1)}, f32[2,6144]{1,0:T(2,128)}, u32[]{:S(2)}) copy-start(f32[2,6144]{1,0:T(2,128)} %param.17) | copy-start | bytes 147460
  142.2 62.4 %all-gather.14.cloned.1.call-start = ((), (), s32[]{:S(2)}) async-start(), calls=%async_computation.3 | async-start | bytes 1966080 | tf_op jit(solution)/shard_map/all_gather | solution.py:91
  142.8 101.5 %all-gather.8.cloned.1.call-start = ((), (), s32[]{:S(2)}) async-start(), calls=%async_computation | async-start | bytes 3538944 | tf_op jit(solution)/shard_map/all_gather | solution.py:84
  244.2 6.9 %copy-start.2 = (f32[49152]{0:T(1024)S(1)}, f32[49152]{0:T(1024)}, u32[]{:S(2)}) copy-start(f32[49152]{0:T(1024)} %all_gather.25) | copy-start | bytes 589828
  294.2 83.5 %copy-start.3 = (f32[49152]{0:T(1024)S(1)}, f32[49152]{0:T(1024)}, u32[]{:S(2)}) copy-start(f32[49152]{0:T(1024)} %all_gather.25) | copy-start | bytes 589828
  294.2 83.5 %copy-start.4 = (f32[49152,2]{0,1:T(2,128)S(1)}, f32[49152,2]{0,1:T(2,128)}, u32[]{:S(2)}) copy-start(f32[49152,2]{0,1:T(2,128)} %get-tuple-element.184) | copy-start | bytes 1179652
Sparse Core Ops, SparseCore 0:
  77.5 60.7 all-reduce.3
Sparse Core Ops, SparseCore 1:
  95.1 31.7 all-gather.11
  142.3 29.8 all-gather.9
  173.8 30.7 all-gather.13
  206.2 38.0 all-gather.7
where the time goes:
time: 389 us; the launch traced here: 387 us
  waiting for transfers between devices  105 us (27%)
  blocking collectives  87 us (22%)
  other arithmetic  73.1 us (19%)
  local copies, waits for them, and re-layouts  54.4 us (14%)
  matrix products  25.3 us (7%)
  loops' own time  22.7 us (6%)
  between operations  19.7 us (5%)
    convert_element_type x32, other arithmetic, unpack_half(): return bit_table.reshape(new_shape).astype(jnp.bfloat16)  55.2 us
    psum x1, waiting for transfers between devices, shards(): aon = lax.psum(partial_value, 'org')  42.7 us
    psum x1, blocking collectives, both_totals(): return lax.psum((cost_part, path_part), ('cls', 'org'))  39.7 us
    all_gather x1, waiting for transfers between devices, shards(): lax.all_gather(interaction, 'org', axis=2, tiled=True)  36 us
    all_gather x3, waiting for transfers between devices, full_cost(): flows_all = lax.all_gather(flow_value, 'cls', axis=0, tiled=True)  24.8 us
    dynamic_slice x32, local copies, waits for them, and re-layouts, fold_links(): lax.scan(advance, skim_carry, jnp.arange(turn_count, dtype=jnp.int32))  18.8 us
    all_gather x1, blocking collectives, shards(): lax.all_gather(flows_start, 'org', axis=1, tiled=True)  17.5 us
    shift_right_arithmetic x96, local copies, waits for them, and re-layouts, unpack_half(): jnp.right_shift(packed[..., :, None, :], shifts[:, None])  17.5 us
  transfers between devices with their start and end apart: 5, of which 3 were waited for; matrix products, arithmetic and copies ran while one was open for 4% of the time, Pallas kernels for 0%

commit v1 on v0

--- a/solution.py
+++ b/solution.py
@@ -6,6 +6,10 @@
 BITS = 30
 ITERS = 2
 HIGH = lax.Precision.HIGHEST
+
+
+def search_hubs(original):
+    return jnp.sum(lax.all_gather(original, "org"), 0)
 
 
 def unpack_half(packed):
@@ -96,7 +100,7 @@
         fold_links = make_fold(incidence[iteration], link_shard)
         skim_now = fold_links(skim_init, cost_now, jnp.int32(0))
         partial_value = anchor_loads_local(incidence[iteration], trips_half, link_shard, org_count)
-        aon = lax.psum(partial_value, "org")
+        aon = search_hubs(partial_value)
         product = lax.dynamic_slice_in_dim(cost_now * flow_now, own_start, link_shard, 1)
         cost_total, path_total = both_totals(jnp.sum(product), jnp.sum(demand_real * skim_now))
         gap_list.append((cost_total - path_total) / cost_total)

time: 389 us -> 403 us (1.036)
  waiting for transfers between devices: 105 us -> 115 us
  other arithmetic: 73.1 us -> 78 us
    psum x1 -> x0, waiting for transfers between devices: 42.7 us -> none  [shards(): aon = lax.psum(partial_value, 'org')]
    all_gather x3, waiting for transfers between devices: 24.8 us -> 52.6 us  [full_cost(): flows_all = lax.all_gather(flow_value, 'cls', axis=0, tiled=True)]
    all_gather x0 -> x2, waiting for transfers between devices: none -> 25.3 us  [search_hubs(): return jnp.sum(lax.all_gather(original, 'org'), 0)]
    reduce_sum x0 -> x2, other arithmetic: none -> 6.09 us  [search_hubs(): return jnp.sum(lax.all_gather(original, 'org'), 0)]
    unnamed x27 -> x31, local copies, waits for them, and re-layouts: 10.4 us -> 10.3 us
  transfers between devices with their start and end apart: 5 -> 6, of which waited for: 3 -> 4; matrix products, arithmetic and copies ran while one was open for 4% -> 11% of each run, Pallas kernels for 0% -> 0%
where the time goes in v1:
time: 403 us; the launch traced here: 402 us
  waiting for transfers between devices  115 us (29%)
  blocking collectives  87.7 us (22%)
  other arithmetic  78 us (19%)
  local copies, waits for them, and re-layouts  54.4 us (13%)
  matrix products  25.3 us (6%)
  loops' own time  22.7 us (6%)
  between operations  18.2 us (5%)
    convert_element_type x32, other arithmetic, unpack_half(): return bit_table.reshape(new_shape).astype(jnp.bfloat16)  55.2 us
    all_gather x3, waiting for transfers between devices, full_cost(): flows_all = lax.all_gather(flow_value, 'cls', axis=0, tiled=True)  52.6 us
    psum x1, blocking collectives, both_totals(): return lax.psum((cost_part, path_part), ('cls', 'org'))  39.6 us
    all_gather x1, waiting for transfers between devices, shards(): lax.all_gather(interaction, 'org', axis=2, tiled=True)  36 us
    all_gather x2, waiting for transfers between devices, search_hubs(): return jnp.sum(lax.all_gather(original, 'org'), 0)  25.3 us
    dynamic_slice x32, local copies, waits for them, and re-layouts, fold_links(): lax.scan(advance, skim_carry, jnp.arange(turn_count, dtype=jnp.int32))  18.8 us
    shift_right_arithmetic x96, local copies, waits for them, and re-layouts, unpack_half(): jnp.right_shift(packed[..., :, None, :], shifts[:, None])  17.5 us
    all_gather x1, blocking collectives, shards(): lax.all_gather(flows_start, 'org', axis=1, tiled=True)  17.3 us
  transfers between devices with their start and end apart: 6, of which 4 were waited for; matrix products, arithmetic and copies ran while one was open for 11% of the time, Pallas kernels for 0%

profile of v1, /device:TPU:0, one launch (start us, length us, event | category | flops | bytes accessed | tf_op | source)
XLA Modules:
  0.0 401.7 jit_solution(4225735668020664349)
XLA Ops:
  10.1 32.3 %while.42 = (s32[]{:T(128)}, f32[8,2,6144]{2,1,0:T(2,128)S(1)}, s32[8]{0:T(128)S(1)}, s32[2,1,2,49152]{3,0,2,1:T(2,128)S(1)}, bf16[2,1,60]{2,0,1:T(2,128)(2,1)S(...) while((s32[]{:T(128)}, f32[8,2,6144]{2,1,0:T(2,128)S(1)}, s32[8]{0:T(128)S(1)}, ...), condition=%wide.region_1.0_spmd, body=%wide.region_0.1_spmd.sunk | while | flops 3686406 | bytes 3392847 | solution.py:50
  11.4 1.7 fusion.79
  15.5 1.7 fusion.79
  19.5 1.7 fusion.79
  23.6 1.7 fusion.79
  27.6 1.7 fusion.79
  31.6 1.7 fusion.79
  35.7 1.7 fusion.79
  43.5 32.3 %while.43 = (s32[]{:T(128)}, f32[8,2,6144]{2,1,0:T(2,128)S(1)}, s32[8]{0:T(128)S(1)}, s32[2,1,2,49152]{3,0,2,1:T(2,128)S(1)}, bf16[2,1,60]{2,0,1:T(2,128)(2,1)S(...) while((s32[]{:T(128)}, f32[8,2,6144]{2,1,0:T(2,128)S(1)}, s32[8]{0:T(128)S(1)}, ...), condition=%wide.region_4.5_spmd, body=%wide.region_3.4_spmd.sunk | while | flops 3686406 | bytes 3392847 | solution.py:50
  44.9 1.7 fusion.83
  48.9 1.7 fusion.83
  53.0 1.7 fusion.83
  57.0 1.7 fusion.83
  65.1 1.7 fusion.83
  69.1 1.7 fusion.83
  76.7 17.3 %all_gather.27 = f32[2,49152]{1,0:T(2,128)} all-gather(f32[2,6144]{1,0:T(2,128)S(1)} %copy-done.9), channel_id=1, replica_groups=mesh['cls'=4,'org'=8] {'org'}, dimensions={1}, use_global_device_ids=true | all-gather | bytes 442368 | tf_op jit(solution)/shard_map/all_gather | solution.py:91
  94.6 3.0 reduce_sum.76
  97.7 25.3 %all-gather.12.cloned.1.call-done = f32[8,2,49152]{2,1,0:T(2,128)} async-done(((f32[1,2,49152]{2,1,0:T(2,128)}), f32[8,2,49152]{2,1,0:T(2,128)}) %all-gather.12.cloned.1.call-update) | async-done | bytes 3145744 | tf_op jit(solution)/shard_map/all_gather | solution.py:12
  123.0 3.0 reduce_sum.77
  126.1 2.6 multiply_add_fusion
  129.9 15.2 %all_gather.33 = f32[49152]{0:T(1024)} all-gather(f32[6144]{0:T(1024)S(1)} %copy-done.11), channel_id=1, replica_groups=mesh['cls'=4,'org'=8] {'org'}, dimensions={0}, use_global_device_ids=true | all-gather | bytes 221184 | tf_op jit(solution)/shard_map/all_gather | solution.py:90
  145.1 15.7 %all_gather.30 = f32[2,49152]{1,0:T(2,128)} all-gather(f32[2,6144]{1,0:T(2,128)S(1)} %copy-done.10), channel_id=1, replica_groups=mesh['cls'=4,'org'=8] {'org'}, dimensions={1}, use_global_device_ids=true | all-gather | bytes 442368 | tf_op jit(solution)/shard_map/all_gather | solution.py:89
  160.7 2.5 reshape.86
  164.7 22.6 %all-gather.16.cloned.1.call-done = f32[4,2,49152]{2,1,0:T(2,128)} async-done(((f32[1,2,49152]{2,1,0:T(2,128)}), f32[4,2,49152]{2,1,0:T(2,128)}) %all-gather.16.cloned.1.call-update) | async-done | bytes 1572880 | tf_op jit(solution)/shard_map/all_gather | solution.py:95
  187.2 2.5 reshape.84
  189.7 30.1 %all-gather.20.cloned.1.call-done = f32[4,2,49152]{2,1,0:T(2,128)} async-done(((f32[1,2,49152]{2,1,0:T(2,128)}), f32[4,2,49152]{2,1,0:T(2,128)}) %all-gather.20.cloned.1.call-update) | async-done | bytes 1572880 | tf_op jit(solution)/shard_map/all_gather | solution.py:95
  219.8 3.7 reshape.88
  223.4 36.0 %all-gather.14.cloned.1.call-done = f32[2,8,49152]{2,1,0:T(8,128)} async-done(((f32[2,8,6144]{2,1,0:T(8,128)}), f32[2,8,49152]{2,1,0:T(8,128)}) %all-gather.14.cloned.1.call-update) | async-done | bytes 3145744 | tf_op jit(solution)/shard_map/all_gather | solution.py:88
  259.5 6.9 %multiply_reduce_fusion.1 = (f32[49152,2]{0,1:T(2,128)S(1)}, f32[49152,2]{0,1:T(2,128)S(1)}, f32[49152,2]{0,1:T(2,128)}) fusion(f32[2,8,49152]{2,1,0:T(8,128)} %all-gather.14.cloned.1.call-done, f32[49152,8]{0,1:T(8,128)S(1)} %bitcast.155, f32[49152,8]{0,1:T(8,128)} %bitcast.157, f32[49152,8]{0,1:T(8,128)S(1)} %bitcast.156), kind=kLoop, calls=%fused_computation.59 | loop fusion | flops 4423680 | bytes 9043968 | tf_op jit(solution)/shard_map/cel,el->cl/dot_general | solution.py:23
  267.8 39.4 %while.44 = (s32[]{:T(128)}, f32[2,1,60]{2,0,1:T(2,128)S(1)}, s32[8]{0:T(128)S(1)}, f32[2,49152]{1,0:T(2,128)S(1)}, s32[2,1,2,49152]{3,0,2,1:T(2,128)}, /*index=5*/s32[]{:T(128)}, s32[1]{0:T(128)}, s32[]{:T(128)}, s32[]{:T(128)}) while((s32[]{:T(128)}, f32[2,1,60]{2,0,1:T(2,128)S(1)}, s32[8]{0:T(128)S(1)}, ...), condition=%wide.region_8.9_spmd.clone, body=%wide.region_6.8_spmd.clone.sunk | while | flops 6943207 | bytes 3615725 | solution.py:66
  308.7 39.4 %while.45 = (s32[]{:T(128)}, f32[2,1,60]{2,0,1:T(2,128)S(1)}, s32[8]{0:T(128)S(1)}, f32[2,49152]{1,0:T(2,128)S(1)}, s32[2,1,2,49152]{3,0,2,1:T(2,128)}, /*index=5*/s32[]{:T(128)}, s32[1]{0:T(128)}, s32[]{:T(128)}, s32[]{:T(128)}) while((s32[]{:T(128)}, f32[2,1,60]{2,0,1:T(2,128)S(1)}, s32[8]{0:T(128)S(1)}, ...), condition=%wide.region_11.12_spmd.clone, body=%wide.region_9.11_spmd.clone.sunk | while | flops 6943207 | bytes 3615725 | solution.py:66
  348.6 39.6 %all-reduce = (f32[]{:T(128)}, f32[]{:T(128)}, f32[]{:T(128)}, f32[]{:T(128)}) all-reduce(f32[]{:T(128)} %fusion.53, f32[]{:T(128)} %get-tuple-element.186, f32[]{:T(128)} %fusion.54, f32[]{:T(128)} %get-tuple-element.185), channel_id=1, replica_groups=mesh['cls'=4,'org'=8] {'cls','org'}, use_global_device_ids=true, to_apply=%region_17.18 | all-reduce | flops 4 | bytes 32 | tf_op jit(solution)/shard_map/psum | solution.py:73
  (354 shorter events, 112.4 us)
Async XLA Ops:
  7.2 1.5 copy-start.13
  7.2 87.4 %all-gather.10.cloned.1.call-start = ((), (), s32[]{:S(2)}) async-start(), calls=%async_computation | async-start | bytes 3538944 | tf_op jit(solution)/shard_map/all_gather | solution.py:12
  42.4 0.7 copy-start.7
  42.4 1.1 copy-start.1
  43.1 79.9 %all-gather.12.cloned.1.call-start = ((), (), s32[]{:S(2)}) async-start(), calls=%async_computation.1 | async-start | bytes 3538944 | tf_op jit(solution)/shard_map/all_gather | solution.py:12
  43.3 33.3 %copy-start.9 = (f32[2,6144]{1,0:T(2,128)S(1)}, f32[2,6144]{1,0:T(2,128)}, u32[]{:S(2)}) copy-start(f32[2,6144]{1,0:T(2,128)} %param.15) | copy-start | bytes 147460
  43.3 50.7 %copy-start.12 = (f32[2]{0:T(128)S(1)}, f32[2]{0:T(128)}, u32[]{:S(2)}) copy-start(f32[2]{0:T(128)} %param.21) | copy-start | bytes 28
  75.8 0.8 copy-start.8
  75.8 21.8 %copy-start = (s32[2,1,2,49152]{3,0,2,1:T(2,128)}, s32[2,1,2,49152]{3,0,2,1:T(2,128)S(1)}, u32[]{:S(2)}) copy-start(s32[2,1,2,49152]{3,0,2,1:T(2,128)S(1)} %get-tuple-element.491) | copy-start | bytes 2359300
  76.6 84.2 %all-gather.18.cloned.1.call-start = ((), (), s32[]{:S(2)}) async-start(), calls=%async_computation.4 | async-start | bytes 1966080 | tf_op jit(solution)/shard_map/all_gather | solution.py:95
  94.0 93.2 %all-gather.16.cloned.1.call-start = ((), (), s32[]{:S(2)}) async-start(), calls=%async_computation.3 | async-start | bytes 1966080 | tf_op jit(solution)/shard_map/all_gather | solution.py:95
  97.7 28.4 %copy-start.2 = (f32[2,49152]{1,0:T(2,128)S(1)}, f32[2,49152]{1,0:T(2,128)}, u32[]{:S(2)}) copy-start(f32[2,49152]{1,0:T(2,128)} %all_gather.27) | copy-start | bytes 1179652
  126.1 3.8 copy-start.11
  126.1 19.0 %copy-start.10 = (f32[2,6144]{1,0:T(2,128)S(1)}, f32[2,6144]{1,0:T(2,128)}, u32[]{:S(2)}) copy-start(f32[2,6144]{1,0:T(2,128)} %param.17) | copy-start | bytes 147460
  128.7 91.1 %all-gather.20.cloned.1.call-start = ((), (), s32[]{:S(2)}) async-start(), calls=%async_computation.5 | async-start | bytes 1966080 | tf_op jit(solution)/shard_map/all_gather | solution.py:95
  129.3 130.2 %all-gather.14.cloned.1.call-start = ((), (), s32[]{:S(2)}) async-start(), calls=%async_computation.2 | async-start | bytes 3538944 | tf_op jit(solution)/shard_map/all_gather | solution.py:88
  259.5 6.9 %copy-start.3 = (f32[2,49152]{1,0:T(2,128)S(1)}, f32[2,49152]{1,0:T(2,128)}, u32[]{:S(2)}) copy-start(f32[2,49152]{1,0:T(2,128)} %all_gather.30) | copy-start | bytes 1179652
  259.5 6.9 %copy-start.4 = (f32[49152]{0:T(1024)S(1)}, f32[49152]{0:T(1024)}, u32[]{:S(2)}) copy-start(f32[49152]{0:T(1024)} %all_gather.33) | copy-start | bytes 589828
  308.6 83.4 %copy-start.5 = (f32[49152]{0:T(1024)S(1)}, f32[49152]{0:T(1024)}, u32[]{:S(2)}) copy-start(f32[49152]{0:T(1024)} %all_gather.33) | copy-start | bytes 589828
  308.6 83.4 %copy-start.6 = (f32[49152,2]{0,1:T(2,128)S(1)}, f32[49152,2]{0,1:T(2,128)}, u32[]{:S(2)}) copy-start(f32[49152,2]{0,1:T(2,128)} %get-tuple-element.184) | copy-start | bytes 1179652
Sparse Core Ops, SparseCore 0:
  43.3 40.9 all-gather.9
  85.9 37.0 all-gather.11
  124.9 29.7 all-gather.17
  156.3 30.8 all-gather.15
  188.9 30.8 all-gather.19
  221.2 38.1 all-gather.13
